TPU v7x, 32 devices: a whole 2x2x4 slice. The times are simulated.
32 devices in a mesh: batch: 8 (over z, x), cols: 4 (over y, core).
Axes of the slice: x: 2, y: 2, z: 4, core: 2. Of those that a mesh axis runs over, the one named last changes fastest.
Arguments:
- partial_query: float32 [8, 1024, 1024], P('batch', None, 'cols'), may hold values from -0.875 to 0.875
- partial_key: float32 [8, 1024, 1024], P('batch', None, 'cols'), may hold values from -0.875 to 0.875
- partial_value: float32 [8, 1024, 1024], P('batch', None, 'cols'), may hold values from -0.875 to 0.875
- partial_mixed: float32 [8, 1024, 1024], P('batch', 'cols'), may hold values from -0.875 to 0.875
- partial_norm: float32 [8, 1024], P('batch'), may hold values from -8 to 8
- partial_bias: float32 [8, 1024], P('batch'), may hold values from -8 to 8
- master_query: float32 [1024, 1024], P('batch', 'cols'), may hold values from -0.1875 to 0.1875
- master_key: float32 [1024, 1024], P('batch', 'cols'), may hold values from -0.1875 to 0.1875
- master_value: float32 [1024, 1024], P('batch', 'cols'), may hold values from -0.1875 to 0.1875
- master_mixed: float32 [1024, 1024], P('cols', 'batch'), may hold values from -0.1875 to 0.1875
- master_norm: float32 [1024], P('batch'), may hold values from 0.25 to 1.75
- master_bias: float32 [1024], P('batch'), may hold values from -3 to 3
Outputs:
- compute_query: bfloat16 [1024, 1024], P(None, 'cols')
- compute_key: bfloat16 [1024, 1024], P(None, 'cols')
- compute_value: bfloat16 [1024, 1024], P(None, 'cols')
- compute_mixed: bfloat16 [1024, 1024], P('cols')
- compute_norm: bfloat16 [1024], replicated
- compute_bias: bfloat16 [1024], replicated
- stepped_query: float32 [1024, 1024], P('batch', 'cols')
- stepped_key: float32 [1024, 1024], P('batch', 'cols')
- stepped_value: float32 [1024, 1024], P('batch', 'cols')
- stepped_mixed: float32 [1024, 1024], P('cols', 'batch')
- stepped_norm: float32 [1024], P('batch')
- stepped_bias: float32 [1024], P('batch')
All inputs are finite; a program needn't handle non-finite values.
Results may differ from a plain program's by a relative error of at most 0.001.
Values may be sent and summed in bfloat16 or wider, within the bound.
A program may use at most 64 MiB of HBM per device.

v0:
```python
import functools

import jax
import jax.numpy as jnp
from jax import lax
from jax.experimental import pallas as pl
from jax.experimental.pallas import tpu as pltpu
from jax.sharding import PartitionSpec as P

learn_rate = 0.4
HALVES = 2
SPAN = 118.0


def encode(x, limit):
    power = jnp.exp2(jnp.abs(x) * (2 * SPAN / limit) - SPAN)
    return jnp.where(x < 0, -power, power).astype(jnp.bfloat16)


def decode(code, limit):
    y = code.astype(jnp.float32)
    size = (jnp.log2(jnp.abs(y)) + SPAN) * (limit / (2 * SPAN))
    return jnp.where(y < 0, -size, size)


def kernel(n, kinds, limit, *refs):
    count = len(kinds)
    groups = n // 2
    refs = list(refs)

    def take(k):
        out = refs[:k]
        del refs[:k]
        return out

    source, master = take(count), take(count)
    norm, bias, norm_master, bias_master = take(4)
    gathered, stepped = take(count), take(count)
    vec_all, vec_mine = take(2)
    pair_out, pair_in, part_out, part_in = take(count), take(count), take(count), take(count)
    own, partial = take(count), take(count)
    vec_out, vec_in = take(2)
    (in_sem,) = take(1)
    a_send, a_recv, b_send, b_recv, c_send, c_recv, d_send, d_recv = take(8)
    v_send, v_recv, w_send, w_recv = take(4)

    rate = n ** (-0.5)
    b = lax.axis_index("batch")
    side = lax.rem(b, 2)
    g = b // 2
    partner = b + 1 - 2 * side

    def remote(src, dst, send, recv, to):
        return pltpu.make_async_remote_copy(
            src_ref=src,
            dst_ref=dst,
            send_sem=send,
            recv_sem=recv,
            device_id={"batch": to},
            device_id_type=pl.DeviceIdType.MESH,
        )

    chunks = [(a, h) for h in range(HALVES) for a in range(count)]

    def place(a, h, d):
        rows, cols = stepped[a].shape
        r = rows // HALVES
        if kinds[a] == "rows":
            return pl.ds(pl.multiple_of(d * rows + h * r, r), r), pl.ds(0, cols)
        return pl.ds(h * r, r), pl.ds(pl.multiple_of(d * cols, cols), cols)

    def load(a, h, d):
        rows, cols = place(a, h, d)
        return partial[a][rows, cols]

    def other(k):
        return lax.rem(g + k, groups)

    loads = [
        pltpu.make_async_copy(source[a].at[0], partial[a], in_sem.at[a])
        for a in range(count)
    ]
    for copy in loads:
        copy.start()

    barrier = pltpu.get_barrier_semaphore()
    for k in range(1, n):
        pl.semaphore_signal(
            barrier,
            inc=1,
            device_id={"batch": lax.rem(b + k, n)},
            device_id_type=pl.DeviceIdType.MESH,
        )

    def pair_encode(c):
        a, h = chunks[c]

        def body(k, carry):
            pair_out[a][h, k] = encode(load(a, h, 2 * k + 1 - side), limit)
            return carry

        lax.fori_loop(0, groups, body, 0)

    def pair_copy(c):
        a, h = chunks[c]
        return remote(
            pair_out[a].at[h], pair_in[a].at[h], a_send.at[c], a_recv.at[c], partner
        )

    def part_copy(c, src_slot, dst_slot, to):
        a, h = chunks[c]
        return remote(
            part_out[a].at[h, src_slot],
            part_in[a].at[h, dst_slot],
            b_send.at[c, src_slot],
            b_recv.at[c, dst_slot],
            2 * to + side,
        )

    def pair_finish(c):
        a, h = chunks[c]
        pair_copy(c).wait_recv()
        for k in range(1, groups):
            to = other(k)
            total = load(a, h, 2 * to + side) + decode(pair_in[a][h, to], limit)
            part_out[a][h, to] = encode(total, 2 * limit)
            part_copy(c, to, g, to).start()
        own[a][h] = load(a, h, b) + decode(pair_in[a][h, g], limit)

    def line_copy(c, owner, way, to=None):
        a, h = chunks[c]
        rows, cols = place(a, h, owner)
        block = gathered[a].at[rows, cols]
        return remote(
            block,
            block,
            c_send.at[(way + 1) // 2, c, owner // 2],
            c_recv.at[c, owner // 2],
            b + 2 * way if to is None else to,
        )

    def has_next(way):
        return g < groups - 1 if way > 0 else g > 0

    def has_source(way, k):
        return g - k >= 0 if way > 0 else g + k < groups

    def cross_copy(c, owner, recv_owner):
        a, h = chunks[c]
        rows, cols = place(a, h, owner)
        block = gathered[a].at[rows, cols]
        return remote(
            block, block, d_send.at[c, owner // 2], d_recv.at[c, recv_owner // 2], partner
        )

    def part_finish(c):
        a, h = chunks[c]
        r = stepped[a].shape[0] // HALVES
        total = own[a][h]
        for k in range(1, groups):
            source = other(k)
            part_copy(c, source, source, source).wait_recv()
            total = total + decode(part_in[a][h, source], 2 * limit)
        rows = pl.ds(h * r, r)
        new = master[a][rows, :] - learn_rate * (total * rate)
        stepped[a][rows, :] = new
        at_rows, at_cols = place(a, h, b)
        gathered[a][at_rows, at_cols] = new.astype(jnp.bfloat16)
        for way in (1, -1):

            @pl.when(has_next(way))
            def _():
                line_copy(c, b, way).start()

        cross_copy(c, b, b).start()

    def line_finish(c, k):
        for way in (1, -1):

            @pl.when(has_source(way, k))
            def _():
                owner = b - 2 * k * way
                line_copy(c, owner, way, owner).wait_recv()

                @pl.when(has_next(way))
                def _():
                    line_copy(c, owner, way).start()

                cross_copy(c, owner, owner).start()

    def vec_copy(k):
        to = lax.rem(b + k, n)
        return remote(vec_out.at[to], vec_in.at[b], v_send.at[to], v_recv.at[b], to)

    def vec_back(k):
        to = lax.rem(b + k, n)
        return remote(vec_all.at[b], vec_all.at[b], w_send.at[to], w_recv.at[b], to)

    loads[0].wait()
    pair_encode(0)
    pl.semaphore_wait(barrier, n - 1)
    pair_copy(0).start()
    for d in range(n):
        vec_out[d, 0:1, :] = norm[d]
        vec_out[d, 1:2, :] = bias[d]
    for k in range(1, n):
        vec_copy(k).start()
    for c in range(1, len(chunks)):
        if c < count:
            loads[c].wait()
        pair_encode(c)
        pair_copy(c).start()

    for t in range(len(chunks) + groups):
        if t < len(chunks):
            pair_finish(t)
        if 0 <= t - 1 < len(chunks):
            part_finish(t - 1)
        if t == 1:
            total = vec_out[b]
            for k in range(1, n):
                source = lax.rem(b + k, n)
                remote(
                    vec_out.at[source],
                    vec_in.at[source],
                    v_send.at[source],
                    v_recv.at[source],
                    source,
                ).wait_recv()
                total = total + vec_in[source]
            mean = total * rate
            vec_mine[0:1, :] = norm_master[...] - learn_rate * mean[0:1]
            vec_mine[1:2, :] = bias_master[...] - learn_rate * mean[1:2]
            vec_all[b] = vec_mine[...]
            for k in range(1, n):
                vec_back(k).start()
        for k in range(groups - 1, 0, -1):
            if 0 <= t - 1 - k < len(chunks):
                line_finish(t - 1 - k, k)

    for c in range(len(chunks)):
        for k in range(groups):
            owner = 2 * other(k) + 1 - side
            cross_copy(c, owner, owner).wait_recv()
    for k in range(1, n):
        source = lax.rem(b + k, n)
        remote(
            vec_all.at[source],
            vec_all.at[source],
            w_send.at[source],
            w_recv.at[source],
            source,
        ).wait_recv()
    for k in range(1, n):
        vec_copy(k).wait_send()
        vec_back(k).wait_send()
    for c in range(len(chunks)):
        pair_copy(c).wait_send()
        for k in range(1, groups):
            to = other(k)
            part_copy(c, to, g, to).wait_send()
        for k in range(groups):
            owner = 2 * other(k) + side
            cross_copy(c, owner, owner).wait_send()
        for way in (1, -1):

            @pl.when(has_next(way))
            def _():
                line_copy(c, b, way).wait_send()

            for k in range(1, groups):

                @pl.when(has_source(way, k) & has_next(way))
                def _():
                    line_copy(c, b - 2 * k * way, way).wait_send()


def hand_over(count, *refs):
    sources, vec_all, vec_mine = refs[:count], refs[count], refs[count + 1]
    targets = refs[count + 2 : 2 * count + 2]
    norm, bias, norm_step, bias_step = refs[2 * count + 2 : 2 * count + 6]
    held = refs[2 * count + 6 : 3 * count + 6]
    in_sem, out_sem = refs[3 * count + 6 :]
    ins = [
        pltpu.make_async_copy(sources[i], held[i], in_sem.at[i]) for i in range(count)
    ]
    outs = [
        pltpu.make_async_copy(held[i], targets[i], out_sem.at[i]) for i in range(count)
    ]
    for copy in ins:
        copy.start()
    norm[...] = vec_all[:, 0, :].astype(jnp.bfloat16)
    bias[...] = vec_all[:, 1, :].astype(jnp.bfloat16)
    norm_step[...] = vec_mine[0:1, :]
    bias_step[...] = vec_mine[1:2, :]
    for i in range(count):
        ins[i].wait()
        outs[i].start()
    for copy in outs:
        copy.wait()


def per_device(
    partial_query,
    partial_key,
    partial_value,
    partial_mixed,
    partial_norm,
    partial_bias,
    master_query,
    master_key,
    master_value,
    master_mixed,
    master_norm,
    master_bias,
):
    n = lax.axis_size("batch")
    groups = n // 2
    limit = 0.875 if n <= 8 else 1.25
    wide = master_mixed.shape[1] % 128 == 0
    kinds = ("rows", "rows", "rows", "cols" if wide else "rows")
    if not wide:
        partial_mixed = jnp.swapaxes(partial_mixed, 1, 2)
        master_mixed = master_mixed.T
    partials = (partial_query, partial_key, partial_value, partial_mixed)
    masters = (master_query, master_key, master_value, master_mixed)
    chunk_count = len(partials) * HALVES
    w = master_norm.shape[0]

    out_shape = [jax.ShapeDtypeStruct(p.shape[1:], jnp.bfloat16) for p in partials]
    out_shape += [jax.ShapeDtypeStruct(m.shape, jnp.float32) for m in masters]
    out_shape += [
        jax.ShapeDtypeStruct((n, 2, w), jnp.float32),
        jax.ShapeDtypeStruct((2, w), jnp.float32),
    ]
    coded = [
        pltpu.VMEM((HALVES, groups, m.shape[0] // HALVES, m.shape[1]), jnp.bfloat16)
        for m in masters
    ]
    owns = [
        pltpu.VMEM((HALVES, m.shape[0] // HALVES, m.shape[1]), jnp.float32)
        for m in masters
    ]
    dma = pltpu.SemaphoreType.DMA
    vmem = pl.BlockSpec(memory_space=pltpu.VMEM)
    hbm = pl.BlockSpec(memory_space=pltpu.HBM)
    outs = pl.pallas_call(
        functools.partial(kernel, n, kinds, limit),
        out_shape=out_shape,
        in_specs=[hbm] * len(partials) + [vmem] * (len(partials) + 4),
        out_specs=[vmem] * len(out_shape),
        scratch_shapes=coded * 4
        + owns
        + [pltpu.VMEM(p.shape[1:], jnp.float32) for p in partials]
        + [pltpu.VMEM((n, 2, w), jnp.float32)] * 2
        + [dma((len(partials),))]
        + [dma((chunk_count,))] * 2
        + [dma((chunk_count, groups))] * 2
        + [dma((2, chunk_count, groups))]
        + [dma((chunk_count, groups))] * 3
        + [dma((n,))] * 4,
        compiler_params=pltpu.CompilerParams(collective_id=0, has_side_effects=True),
    )(
        *partials,
        *masters,
        partial_norm.reshape(n, 1, w),
        partial_bias.reshape(n, 1, w),
        master_norm.reshape(1, w),
        master_bias.reshape(1, w),
    )
    large, (vec_all, vec_mine) = outs[:8], outs[8:]
    tail_shape = [jax.ShapeDtypeStruct(x.shape, x.dtype) for x in large]
    tail_shape += [jax.ShapeDtypeStruct((n, w), jnp.bfloat16)] * 2
    tail_shape += [jax.ShapeDtypeStruct((1, w), jnp.float32)] * 2
    outs = pl.pallas_call(
        functools.partial(hand_over, len(large)),
        out_shape=tail_shape,
        in_specs=[hbm] * len(large) + [vmem] * 2,
        out_specs=[hbm] * len(large) + [vmem] * 4,
        scratch_shapes=[pltpu.VMEM(x.shape, x.dtype) for x in large]
        + [dma((len(large),))] * 2,
    )(*large, vec_all, vec_mine)
    computes, steppeds, vectors = outs[:4], outs[4:8], outs[8:]
    if not wide:
        computes = (*computes[:3], computes[3].T)
        steppeds = (*steppeds[:3], steppeds[3].T)
    norm, bias, norm_step, bias_step = (v.reshape(-1) for v in vectors)
    return (*computes, norm, bias, *steppeds, norm_step, bias_step)


def solution(mesh):
    in_specs = (
        P("batch", None, "cols"),
        P("batch", None, "cols"),
        P("batch", None, "cols"),
        P("batch", "cols", None),
        P("batch", None),
        P("batch", None),
        P("batch", "cols"),
        P("batch", "cols"),
        P("batch", "cols"),
        P("cols", "batch"),
        P("batch"),
        P("batch"),
    )
    out_specs = (
        P(None, "cols"),
        P(None, "cols"),
        P(None, "cols"),
        P("cols", None),
        P(),
        P(),
        P("batch", "cols"),
        P("batch", "cols"),
        P("batch", "cols"),
        P("cols", "batch"),
        P("batch"),
        P("batch"),
    )
    return jax.shard_map(
        per_device, mesh=mesh, in_specs=in_specs, out_specs=out_specs, check_vma=False
    )
```

profile of v0, /device:TPU:0, one launch (start us, length us, event | category | flops | bytes accessed | tf_op | source)
XLA Modules:
  0.0 66.6 jit_solution(16126031741940400865)
XLA Ops:
  0.6 62.0 %shard_map.211 = (bf16[1024,256]{1,0:T(8,128)(2,1)}, bf16[1024,256]{1,0:T(8,128)(2,1)}, bf16[1024,256]{1,0:T(8,128)(2,1)}, bf16[256,1024]{1,0:T(8,128)(2,1)}, f3...) custom-call(f32[1,1024,256]{2,1,0:T(8,128)} %refs_0_.1, ...), custom_call_target="tpu_custom_call" | custom-call | tf_op jit(solution)/shard_map/pallas_call | solution.py:347
  62.7 4.0 %shard_map.212 = (bf16[1024,256]{1,0:T(8,128)(2,1)}, bf16[1024,256]{1,0:T(8,128)(2,1)}, bf16[1024,256]{1,0:T(8,128)(2,1)}, bf16[256,1024]{1,0:T(8,128)(2,1)}, f3...) custom-call(bf16[1024,256]{1,0:T(8,128)(2,1)} %get-tuple-element.34., ...), custom_call_target="tpu_custom_call" | custom-call | tf_op jit(solution)/shard_map/pallas_call | solution.py:375
where the time goes:
time: 66.9 us; the launch traced here: 66.6 us
  Pallas kernels  66 us (99%)
    pallas_call x1, Pallas kernels, per_device(): pl.pallas_call(functools.partial(kernel, n, kinds, limit), out_shape=out_...  62 us
    pallas_call x1, Pallas kernels, per_device(): pl.pallas_call(functools.partial(hand_over, len(large)), out_shape=tail_s...  3.95 us

commit v1 on v0

--- a/solution.py
+++ b/solution.py
@@ -279,23 +279,16 @@
     sources, vec_all, vec_mine = refs[:count], refs[count], refs[count + 1]
     targets = refs[count + 2 : 2 * count + 2]
     norm, bias, norm_step, bias_step = refs[2 * count + 2 : 2 * count + 6]
-    held = refs[2 * count + 6 : 3 * count + 6]
-    in_sem, out_sem = refs[3 * count + 6 :]
-    ins = [
-        pltpu.make_async_copy(sources[i], held[i], in_sem.at[i]) for i in range(count)
+    (out_sem,) = refs[2 * count + 6 :]
+    outs = [
+        pltpu.make_async_copy(sources[i], targets[i], out_sem.at[i]) for i in range(count)
     ]
-    outs = [
-        pltpu.make_async_copy(held[i], targets[i], out_sem.at[i]) for i in range(count)
-    ]
-    for copy in ins:
+    for copy in outs:
         copy.start()
     norm[...] = vec_all[:, 0, :].astype(jnp.bfloat16)
     bias[...] = vec_all[:, 1, :].astype(jnp.bfloat16)
     norm_step[...] = vec_mine[0:1, :]
     bias_step[...] = vec_mine[1:2, :]
-    for i in range(count):
-        ins[i].wait()
-        outs[i].start()
     for copy in outs:
         copy.wait()
 
@@ -344,9 +337,10 @@
     dma = pltpu.SemaphoreType.DMA
     vmem = pl.BlockSpec(memory_space=pltpu.VMEM)
     hbm = pl.BlockSpec(memory_space=pltpu.HBM)
+    pin = lambda x: pltpu.with_memory_space_constraint(x, pltpu.HBM)
     outs = pl.pallas_call(
         functools.partial(kernel, n, kinds, limit),
-        out_shape=out_shape,
+        out_shape=[pltpu.VMEM(x.shape, x.dtype) for x in out_shape],
         in_specs=[hbm] * len(partials) + [vmem] * (len(partials) + 4),
         out_specs=[vmem] * len(out_shape),
         scratch_shapes=coded * 4
@@ -359,14 +353,14 @@
         + [dma((2, chunk_count, groups))]
         + [dma((chunk_count, groups))] * 3
         + [dma((n,))] * 4,
-        compiler_params=pltpu.CompilerParams(collective_id=0, has_side_effects=True),
+        compiler_params=pltpu.CompilerParams(collective_id=0, has_side_effects=True, vmem_limit_bytes=40 << 20),
     )(
-        *partials,
-        *masters,
-        partial_norm.reshape(n, 1, w),
-        partial_bias.reshape(n, 1, w),
-        master_norm.reshape(1, w),
-        master_bias.reshape(1, w),
+        *(pin(x) for x in partials),
+        *(pin(x) for x in masters),
+        pin(partial_norm.reshape(n, 1, w)),
+        pin(partial_bias.reshape(n, 1, w)),
+        pin(master_norm.reshape(1, w)),
+        pin(master_bias.reshape(1, w)),
     )
     large, (vec_all, vec_mine) = outs[:8], outs[8:]
     tail_shape = [jax.ShapeDtypeStruct(x.shape, x.dtype) for x in large]
@@ -375,11 +369,11 @@
     outs = pl.pallas_call(
         functools.partial(hand_over, len(large)),
         out_shape=tail_shape,
-        in_specs=[hbm] * len(large) + [vmem] * 2,
+        in_specs=[vmem] * (len(large) + 2),
         out_specs=[hbm] * len(large) + [vmem] * 4,
-        scratch_shapes=[pltpu.VMEM(x.shape, x.dtype) for x in large]
-        + [dma((len(large),))] * 2,
-    )(*large, vec_all, vec_mine)
+        scratch_shapes=[dma((len(large),))],
+        compiler_params=pltpu.CompilerParams(vmem_limit_bytes=8 << 20),
+    )(*(pltpu.with_memory_space_constraint(x, pltpu.VMEM) for x in (*large, vec_all, vec_mine)))
     computes, steppeds, vectors = outs[:4], outs[4:8], outs[8:]
     if not wide:
         computes = (*computes[:3], computes[3].T)

time: 66.9 us -> 63.5 us (0.949)
  Pallas kernels: 66 us -> 62.7 us
    pallas_call x1, Pallas kernels: 3.95 us -> 2.15 us  [per_device(): pl.pallas_call(functools.partial(hand_over, len(large)), out_shape=tail_s...]
    pallas_call x1, Pallas kernels: 62 us -> 60.5 us  [per_device(): pl.pallas_call(functools.partial(kernel, n, kinds, limit), out_shape=[plt...]
where the time goes in v1:
time: 63.5 us; the launch traced here: 63.4 us
  Pallas kernels  62.7 us (99%)
  between operations  0.66 us (1%)
    pallas_call x1, Pallas kernels, per_device(): pl.pallas_call(functools.partial(kernel, n, kinds, limit), out_shape=[plt...  60.5 us
    pallas_call x1, Pallas kernels, per_device(): pl.pallas_call(functools.partial(hand_over, len(large)), out_shape=tail_s...  2.15 us

profile of v1, /device:TPU:0, one launch (start us, length us, event | category | flops | bytes accessed | tf_op | source)
XLA Modules:
  0.0 63.4 jit_solution(462661022529939443)
XLA Ops:
  0.6 60.5 %shard_map.211 = (bf16[1024,256]{1,0:T(8,128)(2,1)S(1)}, bf16[1024,256]{1,0:T(8,128)(2,1)S(1)}, bf16[1024,256]{1,0:T(8,128)(2,1)S(1)}, bf16[256,1024]{1,0:T(8,12...) custom-call(f32[1,1024,256]{2,1,0:T(8,128)} %refs_0_.1, ...), custom_call_target="tpu_custom_call" | custom-call | tf_op jit(solution)/shard_map/pallas_call | solution.py:341
  61.2 2.1 %shard_map.212 = (bf16[1024,256]{1,0:T(8,128)(2,1)}, bf16[1024,256]{1,0:T(8,128)(2,1)}, bf16[1024,256]{1,0:T(8,128)(2,1)}, bf16[256,1024]{1,0:T(8,128)(2,1)}, f3...) custom-call(bf16[1024,256]{1,0:T(8,128)(2,1)S(1)} %get-tuple-element, ...), custom_call_target="tpu_custom_call" | custom-call | tf_op jit(solution)/shard_map/pallas_call | solution.py:369

commit v2 on v1

--- a/solution.py
+++ b/solution.py
@@ -9,7 +9,145 @@
 
 learn_rate = 0.4
 HALVES = 2
-SPAN = 118.0
+SPAN = 125.0
+
+PLAN = (
+    (0, 0, 4, "Z", "Z"),
+    (0, 4, 4, "Z", "Z"),
+    (1, 0, 4, "X", "X"),
+    (1, 4, 4, "X", "X"),
+    (2, 0, 4, "X", "X"),
+    (2, 4, 4, "X", "X"),
+    (3, 0, 4, "X", "X"),
+    (3, 4, 4, "X", "X"),
+)
+ORDERS = (
+    (
+        "0:z0",
+        "6:x1",
+        "8:x1",
+        "1:z0",
+        "7:x1",
+        "5:x1",
+        "8:z0",
+        "6:z0",
+        "7:z0",
+        "2:x1",
+        "3:x1",
+        "5:z0",
+        "4:x1",
+        "2:z0",
+        "0:zf",
+        "3:z0",
+        "4:z0",
+        "1:zf",
+        "0:f",
+        "6:f",
+        "5:r1",
+        "5:f",
+        "1:f",
+        "8:f",
+        "2:f",
+        "6:r1",
+        "7:r1",
+        "0:b0",
+        "7:f",
+        "6:r2",
+        "1:b0",
+        "7:r2",
+        "3:f",
+        "5:r2",
+        "4:f",
+        "4:r1",
+        "3:r1",
+        "2:r1",
+        "8:r3",
+        "6:r3",
+        "8:r1",
+        "4:r2",
+        "2:r3",
+        "3:r2",
+        "2:r2",
+        "5:r3",
+        "3:r3",
+        "7:r3",
+        "8:r2",
+        "4:r3",
+    ),
+    (
+        "5:x1",
+        "6:x1",
+        "8:x1",
+        "7:x1",
+        "2:x1",
+        "4:x1",
+        "0:a",
+        "1:a",
+        "6:a",
+        "3:x1",
+        "0:b",
+        "0:zf",
+        "7:a",
+        "8:a",
+        "1:b",
+        "5:a",
+        "1:zf",
+        "6:b",
+        "6:f",
+        "7:b",
+        "2:a",
+        "7:f",
+        "0:f",
+        "5:f",
+        "5:b",
+        "3:a",
+        "8:b",
+        "6:rM",
+        "2:b",
+        "0:b0",
+        "8:f",
+        "4:a",
+        "7:rM",
+        "5:rM",
+        "2:f",
+        "3:b",
+        "3:f",
+        "6:rE",
+        "1:f",
+        "4:b",
+        "4:f",
+        "1:rE",
+        "8:rE",
+        "2:rM",
+        "5:rE",
+        "6:rF",
+        "3:rM",
+        "2:rE",
+        "1:b0",
+        "0:sE",
+        "0:rM",
+        "3:rE",
+        "8:rF",
+        "4:rM",
+        "2:rF",
+        "0:sM",
+        "5:rF",
+        "7:rE",
+        "4:rE",
+        "1:sE",
+        "1:rM",
+        "3:rF",
+        "8:rM",
+        "7:rF",
+        "0:rE",
+        "4:rF",
+        "0:sF",
+        "1:sF",
+        "1:rF",
+        "0:rF",
+        "1:sM",
+    ),
+)
 
 
 def encode(x, limit):
@@ -275,6 +413,343 @@
                     line_copy(c, b - 2 * k * way, way).wait_send()
 
 
+def ladder(n, kinds, limit, plan, orders, *refs):
+    count = len(kinds)
+    groups = n // 2
+    tiny = len(plan) - 1
+    refs = list(refs)
+
+    def take(k):
+        out = refs[:k]
+        del refs[:k]
+        return out
+
+    source, master_in = take(count), take(count)
+    norm, bias, norm_in, bias_in = take(4)
+    gathered, stepped = take(count), take(count)
+    vec_all, vec_mine = take(2)
+    chunks = len(plan)
+    x1_out, x1_in = take(chunks), take(chunks)
+    z_out, far_in, near_in = take(chunks), take(chunks), take(chunks)
+    x2_out, x2_in, own = take(chunks), take(chunks), take(chunks)
+    partial, master = take(count), take(count)
+    vec_part, norm_part, bias_part, norm_master, bias_master = take(5)
+    in_sem, master_sem, small_sem = take(3)
+    x1_send, x1_recv, x2_send, x2_recv = take(4)
+    z_send, z_recv, g_send, g_recv = take(4)
+
+    rate = n ** (-0.5)
+    b = lax.axis_index("batch")
+    side = lax.rem(b, 2)
+    g = b // 2
+    partner = b + 1 - 2 * side
+    way = jnp.where(g < groups // 2, 1, -1)
+    is_end = (g == 0) | (g == groups - 1)
+
+    loads = [
+        pltpu.make_async_copy(source[a].at[0], partial[a], in_sem.at[a])
+        for a in range(count)
+    ]
+    masters = [
+        pltpu.make_async_copy(master_in[a], master[a], master_sem.at[a])
+        for a in range(count)
+    ]
+    smalls = [
+        pltpu.make_async_copy(src, dst, small_sem.at[i])
+        for i, (src, dst) in enumerate(
+            (
+                (norm, norm_part),
+                (bias, bias_part),
+                (norm_in, norm_master),
+                (bias_in, bias_master),
+            )
+        )
+    ]
+
+    def remote(src, dst, send, recv, to):
+        return pltpu.make_async_remote_copy(
+            src_ref=src,
+            dst_ref=dst,
+            send_sem=send,
+            recv_sem=recv,
+            device_id={"batch": to},
+            device_id_type=pl.DeviceIdType.MESH,
+        )
+
+    def place(c, d):
+        a, start, size = plan[c][:3]
+        rows, cols = stepped[a].shape
+        if kinds[a] == "rows":
+            return pl.ds(pl.multiple_of(d * rows + start, 16), size), pl.ds(0, cols)
+        return pl.ds(start, size), pl.ds(pl.multiple_of(d * cols, cols), cols)
+
+    def load(c, d):
+        if c == tiny:
+            return vec_part[d]
+        rows, cols = place(c, d)
+        return partial[plan[c][0]][rows, cols]
+
+    def block(c, d):
+        if c == tiny:
+            return vec_all.at[d]
+        rows, cols = place(c, d)
+        return gathered[plan[c][0]].at[rows, cols]
+
+    def pack(c, x, terms):
+        return x if c == tiny else encode(x, terms * limit)
+
+    def unpack(c, code, terms):
+        return code if c == tiny else decode(code, terms * limit)
+
+    def x1_copy(c):
+        return remote(x1_out[c], x1_in[c], x1_send.at[c], x1_recv.at[c], partner)
+
+    def x2_copy(c):
+        return remote(x2_out[c], x2_in[c], x2_send.at[c], x2_recv.at[c], partner)
+
+    def program(end, order):
+        waited = set()
+        sent = []
+        met = []
+        out_to = b + 2 * way
+        near_to = b - 2 * way
+        lines = ("out",) if end else ("near", "out")
+
+        def first(key, wait):
+            if key not in waited:
+                waited.add(key)
+                wait()
+
+        def send(copy):
+            if not met:
+                met.append(True)
+                pl.semaphore_wait(barrier, 2 if end else 3)
+            copy.start()
+            sent.append(copy)
+
+        def need(c):
+            if c < tiny:
+                first(("load", plan[c][0]), loads[plan[c][0]].wait)
+                return
+
+            def gather():
+                for copy in smalls:
+                    copy.wait()
+                for d in range(n):
+                    vec_part[d, 0:1, :] = norm_part[d]
+                    vec_part[d, 1:2, :] = bias_part[d]
+
+            first("small", gather)
+
+        def z_copy(c, kind):
+            m = 2 if plan[c][3] == "Z" else 1
+            if kind == "end":
+                lo, size, slot, dst, to = 0, 3 * m, 0, far_in[c], out_to
+            elif kind == "mid":
+                dst = near_in[c].at[pl.ds(0, 2 * m)]
+                lo, size, slot, to = 0, 2 * m, 0, out_to
+            else:
+                dst = near_in[c].at[pl.ds(0, m)]
+                lo, size, slot, to = 2 * m, m, 1, near_to
+            return remote(
+                z_out[c].at[pl.ds(lo, size)],
+                dst,
+                z_send.at[slot, c],
+                z_recv.at[0 if kind == "end" else 1, c],
+                to,
+            )
+
+        def got_far(c):
+            first(("far", c), z_copy(c, "end").wait_recv)
+
+        def got_near(c):
+            first(("near", c), z_copy(c, "back" if end else "mid").wait_recv)
+
+        def got_x1(c):
+            first(("x1", c), x1_copy(c).wait_recv)
+
+        def pair(c, z):
+            return load(c, 2 * z + side) + unpack(c, x1_in[c][z], 1)
+
+        def each(lo, hi, fn):
+            def body(j, carry):
+                fn(j)
+                return carry
+
+            lax.fori_loop(lo, hi, body, 0)
+
+        def x1(c):
+            need(c)
+
+            def put(z):
+                x1_out[c][z] = pack(c, load(c, 2 * z + 1 - side), 1)
+
+            each(0, groups, put)
+            send(x1_copy(c))
+
+        def z0(c):
+            need(c)
+            if plan[c][3] == "Z":
+
+                def put(j):
+                    d = 2 * (g + way * (j // 2 + 1)) + lax.rem(j, 2)
+                    z_out[c][j] = pack(c, load(c, d), 1)
+
+                each(0, 6, put)
+            else:
+                got_x1(c)
+
+                def put(j):
+                    z_out[c][j] = pack(c, pair(c, g + way * (j + 1)), 2)
+
+                each(0, 3, put)
+            send(z_copy(c, "end"))
+
+        def a(c):
+            need(c)
+            if plan[c][3] == "Z":
+                got_far(c)
+
+                def put(j):
+                    d = 2 * (g + way * (j // 2 + 1)) + lax.rem(j, 2)
+                    total = load(c, d) + unpack(c, far_in[c][j + 2], 1)
+                    z_out[c][j] = pack(c, total, 2)
+
+                each(0, 4, put)
+            else:
+                got_x1(c)
+                got_far(c)
+
+                def put(j):
+                    total = pair(c, g + way * (j + 1)) + unpack(c, far_in[c][j + 1], 2)
+                    z_out[c][j] = pack(c, total, 4)
+
+                each(0, 2, put)
+            send(z_copy(c, "mid"))
+
+        def back(c):
+            need(c)
+            z = g - way
+            if plan[c][3] == "Z":
+                got_near(c)
+
+                def put(s):
+                    total = load(c, 2 * z + s) + unpack(c, near_in[c][2 + s], 2)
+                    z_out[c][4 + s] = pack(c, total, 3)
+
+                each(0, 2, put)
+            else:
+                got_x1(c)
+                got_near(c)
+                total = pair(c, z) + unpack(c, near_in[c][1], 4)
+                z_out[c][2] = pack(c, total, 6)
+            send(z_copy(c, "back"))
+
+        def line_sum(c, s):
+            total = load(c, 2 * g + s)
+            if end:
+                return total + unpack(c, near_in[c][s], 3)
+            return total + unpack(c, far_in[c][s], 1) + unpack(c, near_in[c][s], 2)
+
+        def zf(c):
+            need(c)
+            got_near(c)
+            if not end:
+                got_far(c)
+            x2_out[c][...] = pack(c, line_sum(c, 1 - side), 4)
+            send(x2_copy(c))
+            own[c][...] = line_sum(c, side)
+
+        def block_copy(c, d, lane):
+            to = {"x": partner, "out": out_to, "near": near_to}[lane]
+            slot = {"x": 0, "out": 1, "near": 2}[lane]
+            ref = block(c, d)
+            return remote(ref, ref, g_send.at[slot, c, d], g_recv.at[c, d], to)
+
+        def got(c, step, s):
+            d = 2 * (g + way * step) + (1 - side if s else side)
+            first(("block", c, step, s), block_copy(c, d, "x").wait_recv)
+            return d
+
+        def f(c):
+            need(c)
+            if plan[c][3] == "Z":
+                x2_copy(c).wait_recv()
+                total = own[c][...] + unpack(c, x2_in[c][...], 4)
+            else:
+                got_x1(c)
+                got_near(c)
+                total = pair(c, g)
+                if end:
+                    total = total + unpack(c, near_in[c][0], 6)
+                else:
+                    got_far(c)
+                    total = total + unpack(c, far_in[c][0], 2)
+                    total = total + unpack(c, near_in[c][0], 4)
+            if c == tiny:
+                mean = total * rate
+                vec_mine[0:1, :] = norm_master[...] - learn_rate * mean[0:1]
+                vec_mine[1:2, :] = bias_master[...] - learn_rate * mean[1:2]
+                vec_all[b] = vec_mine[...]
+            else:
+                k, start, size = plan[c][:3]
+                first(("master", k), masters[k].wait)
+                rows = pl.ds(start, size)
+                new = master[k][rows, :] - learn_rate * (total * rate)
+                stepped[k][rows, :] = new
+                at_rows, at_cols = place(c, b)
+                gathered[k][at_rows, at_cols] = new.astype(jnp.bfloat16)
+            for lane in lines + ("x",):
+                send(block_copy(c, b, lane))
+
+        def relay(step, s, lanes):
+            def go(c):
+                d = got(c, step, s)
+                for lane in lanes if plan[c][4] == "Z" else lanes + ("x",):
+                    send(block_copy(c, d, lane))
+
+            return go
+
+        moves = {"x1": x1, "z0": z0, "a": a, "b": back, "zf": zf, "f": f}
+        moves["b0"] = relay(0, 1, lines)
+        for step in (1, 2, 3):
+            moves[f"r{step}"] = relay(step, 0, ())
+        for name, step, lane in (("E", -1, "out"), ("M", 1, "near"), ("F", 2, "near")):
+            moves["r" + name] = relay(step, 0, (lane,))
+            moves["s" + name] = relay(step, 1, (lane,))
+
+        for to in (partner, out_to) if end else (partner, out_to, near_to):
+            pl.semaphore_signal(
+                barrier,
+                inc=1,
+                device_id={"batch": to},
+                device_id_type=pl.DeviceIdType.MESH,
+            )
+        for k in dict.fromkeys(plan[c][0] for c, _ in order if c < tiny):
+            loads[k].start()
+        for copy in smalls + masters:
+            copy.start()
+        for c, move in order:
+            moves[move](c)
+        for c in range(chunks):
+            for step in (0, 1, 2, 3) if end else (-1, 0, 1, 2):
+                for s in range(2):
+                    if step or s:
+                        got(c, step, s)
+        for copy in sent:
+            copy.wait_send()
+
+    barrier = pltpu.get_barrier_semaphore()
+
+    @pl.when(is_end)
+    def _():
+        program(True, orders[0])
+
+    @pl.when(jnp.logical_not(is_end))
+    def _():
+        program(False, orders[1])
+
+
 def hand_over(count, *refs):
     sources, vec_all, vec_mine = refs[:count], refs[count], refs[count + 1]
     targets = refs[count + 2 : 2 * count + 2]
@@ -291,6 +766,58 @@
     bias_step[...] = vec_mine[1:2, :]
     for copy in outs:
         copy.wait()
+
+
+def exchange_ladder(partials, masters, vectors, limit, kinds):
+    n = lax.axis_size("batch")
+    groups = n // 2
+    w = vectors[-1].shape[1]
+    plan = []
+    for a, start, size, reduce_kind, gather_kind in PLAN:
+        rows = masters[a].shape[0]
+        plan.append((a, start * rows // 8, size * rows // 8, reduce_kind, gather_kind))
+    shapes = [(size, masters[a].shape[1]) for a, _, size, _, _ in plan] + [(2, w)]
+    types = [jnp.bfloat16] * len(plan) + [jnp.float32]
+    plan.append((None, 0, 2, "X", "X"))
+    orders = [
+        [(int(c), move) for c, move in (step.split(":") for step in order)]
+        for order in ORDERS
+    ]
+
+    def buffers(lead):
+        return [pltpu.VMEM((*lead(p), *s), t) for p, s, t in zip(plan, shapes, types)]
+
+    def line(k):
+        return buffers(lambda p: (2 * k if p[3] == "Z" else k,))
+
+    dma = pltpu.SemaphoreType.DMA
+    chunks = len(plan)
+    out_shape = [pltpu.VMEM(p.shape[1:], jnp.bfloat16) for p in partials]
+    out_shape += [pltpu.VMEM(m.shape, jnp.float32) for m in masters]
+    out_shape += [pltpu.VMEM((n, 2, w), jnp.float32), pltpu.VMEM((2, w), jnp.float32)]
+    scratch = buffers(lambda p: (groups if p[3] == "X" else 1,)) * 2
+    scratch += line(3) * 2 + line(2)
+    scratch += buffers(lambda p: ()) * 2
+    scratch += [pltpu.VMEM(s, jnp.float32) for s in shapes]
+    scratch += [pltpu.VMEM(p.shape[1:], jnp.float32) for p in partials]
+    scratch += [pltpu.VMEM(m.shape, jnp.float32) for m in masters]
+    scratch += [pltpu.VMEM((n, 2, w), jnp.float32)]
+    scratch += [pltpu.VMEM((n, 1, w), jnp.float32)] * 2
+    scratch += [pltpu.VMEM((1, w), jnp.float32)] * 2
+    scratch += [dma((len(partials),))] * 2 + [dma((4,))]
+    scratch += [dma((chunks,))] * 4 + [dma((2, chunks))] * 2
+    scratch += [dma((3, chunks, n)), dma((chunks, n))]
+    args = (*partials, *masters, *vectors)
+    return pl.pallas_call(
+        functools.partial(ladder, n, kinds, limit, plan, orders),
+        out_shape=out_shape,
+        in_specs=[pl.BlockSpec(memory_space=pltpu.HBM)] * len(args),
+        out_specs=[pl.BlockSpec(memory_space=pltpu.VMEM)] * len(out_shape),
+        scratch_shapes=scratch,
+        compiler_params=pltpu.CompilerParams(
+            collective_id=0, has_side_effects=True, vmem_limit_bytes=40 << 20
+        ),
+    )(*(pltpu.with_memory_space_constraint(x, pltpu.HBM) for x in args))
 
 
 def per_device(
@@ -338,7 +865,7 @@
     vmem = pl.BlockSpec(memory_space=pltpu.VMEM)
     hbm = pl.BlockSpec(memory_space=pltpu.HBM)
     pin = lambda x: pltpu.with_memory_space_constraint(x, pltpu.HBM)
-    outs = pl.pallas_call(
+    exchange = pl.pallas_call(
         functools.partial(kernel, n, kinds, limit),
         out_shape=[pltpu.VMEM(x.shape, x.dtype) for x in out_shape],
         in_specs=[hbm] * len(partials) + [vmem] * (len(partials) + 4),
@@ -354,14 +881,17 @@
         + [dma((chunk_count, groups))] * 3
         + [dma((n,))] * 4,
         compiler_params=pltpu.CompilerParams(collective_id=0, has_side_effects=True, vmem_limit_bytes=40 << 20),
-    )(
-        *(pin(x) for x in partials),
-        *(pin(x) for x in masters),
-        pin(partial_norm.reshape(n, 1, w)),
-        pin(partial_bias.reshape(n, 1, w)),
-        pin(master_norm.reshape(1, w)),
-        pin(master_bias.reshape(1, w)),
     )
+    vectors = (
+        partial_norm.reshape(n, 1, w),
+        partial_bias.reshape(n, 1, w),
+        master_norm.reshape(1, w),
+        master_bias.reshape(1, w),
+    )
+    if n == 8 and wide and all(m.shape[0] % 128 == 0 for m in masters):
+        outs = exchange_ladder(partials, masters, vectors, limit, kinds)
+    else:
+        outs = exchange(*(pin(x) for x in (*partials, *masters, *vectors)))
     large, (vec_all, vec_mine) = outs[:8], outs[8:]
     tail_shape = [jax.ShapeDtypeStruct(x.shape, x.dtype) for x in large]
     tail_shape += [jax.ShapeDtypeStruct((n, w), jnp.bfloat16)] * 2

time: 63.5 us -> 56.8 us (0.89)
  Pallas kernels: 62.7 us -> 55.9 us
    pallas_call x1, Pallas kernels: 60.5 us -> 53.8 us  [exchange_ladder(): pl.pallas_call(functools.partial(ladder, n, kinds, limit, plan, orders),...]
where the time goes in v2:
time: 56.8 us; the launch traced here: 56.6 us
  Pallas kernels  55.9 us (98%)
  between operations  0.66 us (1%)
    pallas_call x1, Pallas kernels, exchange_ladder(): pl.pallas_call(functools.partial(ladder, n, kinds, limit, plan, orders),...  53.8 us
    pallas_call x1, Pallas kernels, per_device(): pl.pallas_call(functools.partial(hand_over, len(large)), out_shape=tail_s...  2.15 us

profile of v2, /device:TPU:0, one launch (start us, length us, event | category | flops | bytes accessed | tf_op | source)
XLA Modules:
  0.0 56.6 jit_solution(8352412624725321968)
XLA Ops:
  0.6 53.8 %shard_map.211 = (bf16[1024,256]{1,0:T(8,128)(2,1)S(1)}, bf16[1024,256]{1,0:T(8,128)(2,1)S(1)}, bf16[1024,256]{1,0:T(8,128)(2,1)S(1)}, bf16[256,1024]{1,0:T(8,12...) custom-call(f32[1,1024,256]{2,1,0:T(8,128)} %refs_0_.1, ...), custom_call_target="tpu_custom_call" | custom-call | tf_op jit(solution)/shard_map/pallas_call | solution.py:811
  54.5 2.1 %shard_map.212 = (bf16[1024,256]{1,0:T(8,128)(2,1)}, bf16[1024,256]{1,0:T(8,128)(2,1)}, bf16[1024,256]{1,0:T(8,128)(2,1)}, bf16[256,1024]{1,0:T(8,128)(2,1)}, f3...) custom-call(bf16[1024,256]{1,0:T(8,128)(2,1)S(1)} %get-tuple-element, ...), custom_call_target="tpu_custom_call" | custom-call | tf_op jit(solution)/shard_map/pallas_call | solution.py:899

commit v3 on v2

--- a/solution.py
+++ b/solution.py
@@ -10,10 +10,12 @@
 learn_rate = 0.4
 HALVES = 2
 SPAN = 125.0
+PIECES = 2
 
 PLAN = (
     (0, 0, 4, "Z", "Z"),
-    (0, 4, 4, "Z", "Z"),
+    (0, 4, 2, "Z", "Z"),
+    (0, 6, 2, "X", "X"),
     (1, 0, 4, "X", "X"),
     (1, 4, 4, "X", "X"),
     (2, 0, 4, "X", "X"),
@@ -23,129 +25,142 @@
 )
 ORDERS = (
     (
-        "0:z0",
-        "6:x1",
-        "8:x1",
+        "9:x1",
+        "4:x1",
         "1:z0",
         "7:x1",
+        "2:x1",
         "5:x1",
+        "0:z0",
+        "8:x1",
+        "6:x1",
+        "4:z0",
+        "7:z0",
+        "2:z0",
+        "3:x1",
+        "9:z0",
+        "5:z0",
+        "1:zf",
         "8:z0",
         "6:z0",
-        "7:z0",
-        "2:x1",
-        "3:x1",
-        "5:z0",
-        "4:x1",
-        "2:z0",
+        "4:f",
         "0:zf",
         "3:z0",
-        "4:z0",
-        "1:zf",
+        "1:f",
+        "7:f",
+        "7:r1",
         "0:f",
-        "6:f",
+        "2:f",
         "5:r1",
         "5:f",
-        "1:f",
+        "4:r2",
+        "2:r2",
+        "2:r1",
+        "4:r1",
+        "9:f",
+        "1:b0",
         "8:f",
-        "2:f",
+        "7:r2",
+        "5:r2",
+        "8:r1",
+        "6:f",
+        "3:f",
+        "9:r2",
         "6:r1",
-        "7:r1",
         "0:b0",
-        "7:f",
+        "8:r2",
         "6:r2",
-        "1:b0",
-        "7:r2",
-        "3:f",
-        "5:r2",
-        "4:f",
-        "4:r1",
         "3:r1",
-        "2:r1",
+        "5:r3",
+        "2:r3",
+        "4:r3",
+        "9:r3",
+        "9:r1",
+        "7:r3",
         "8:r3",
         "6:r3",
-        "8:r1",
-        "4:r2",
-        "2:r3",
         "3:r2",
-        "2:r2",
-        "5:r3",
         "3:r3",
-        "7:r3",
-        "8:r2",
-        "4:r3",
     ),
     (
+        "4:x1",
+        "9:x1",
+        "7:x1",
         "5:x1",
+        "1:a",
+        "1:zf",
+        "0:a",
+        "1:b",
+        "2:x1",
+        "8:x1",
         "6:x1",
-        "8:x1",
-        "7:x1",
-        "2:x1",
-        "4:x1",
-        "0:a",
-        "1:a",
-        "6:a",
+        "4:a",
+        "1:f",
+        "7:a",
+        "0:b",
+        "2:a",
+        "9:a",
+        "0:zf",
+        "4:f",
+        "4:b",
+        "1:rM",
         "3:x1",
-        "0:b",
-        "0:zf",
-        "7:a",
+        "5:a",
+        "7:b",
+        "2:f",
+        "9:b",
+        "2:b",
+        "1:b0",
+        "7:f",
+        "4:rM",
         "8:a",
-        "1:b",
-        "5:a",
-        "1:zf",
-        "6:b",
-        "6:f",
-        "7:b",
-        "2:a",
-        "7:f",
-        "0:f",
         "5:f",
         "5:b",
+        "0:f",
+        "1:sM",
+        "2:rM",
+        "6:a",
+        "8:f",
+        "8:b",
+        "5:rM",
+        "7:rM",
         "3:a",
-        "8:b",
+        "6:b",
+        "9:f",
+        "6:f",
+        "4:rE",
+        "8:rM",
+        "5:rE",
+        "3:b",
+        "9:rM",
+        "2:rE",
+        "9:rE",
+        "3:f",
+        "7:rE",
+        "8:rE",
         "6:rM",
-        "2:b",
         "0:b0",
-        "8:f",
-        "4:a",
-        "7:rM",
-        "5:rM",
-        "2:f",
-        "3:b",
-        "3:f",
+        "2:rF",
+        "5:rF",
         "6:rE",
-        "1:f",
-        "4:b",
-        "4:f",
+        "4:rF",
+        "9:rF",
+        "7:rF",
+        "1:sE",
         "1:rE",
-        "8:rE",
-        "2:rM",
-        "5:rE",
+        "8:rF",
+        "3:rE",
+        "0:rE",
         "6:rF",
         "3:rM",
-        "2:rE",
-        "1:b0",
         "0:sE",
-        "0:rM",
-        "3:rE",
-        "8:rF",
-        "4:rM",
-        "2:rF",
         "0:sM",
-        "5:rF",
-        "7:rE",
-        "4:rE",
-        "1:sE",
-        "1:rM",
         "3:rF",
-        "8:rM",
-        "7:rF",
-        "0:rE",
-        "4:rF",
+        "0:rF",
+        "1:rF",
         "0:sF",
         "1:sF",
-        "1:rF",
-        "0:rF",
-        "1:sM",
+        "0:rM",
     ),
 )
 
@@ -427,16 +442,15 @@
     source, master_in = take(count), take(count)
     norm, bias, norm_in, bias_in = take(4)
     gathered, stepped = take(count), take(count)
-    vec_all, vec_mine = take(2)
+    norm_out, bias_out, norm_step, bias_step = take(4)
     chunks = len(plan)
     x1_out, x1_in = take(chunks), take(chunks)
     z_out, far_in, near_in = take(chunks), take(chunks), take(chunks)
     x2_out, x2_in, own = take(chunks), take(chunks), take(chunks)
     partial, master = take(count), take(count)
-    vec_part, norm_part, bias_part, norm_master, bias_master = take(5)
+    vec_all, vec_part, norm_part, bias_part, norm_master, bias_master = take(6)
     in_sem, master_sem, small_sem = take(3)
-    x1_send, x1_recv, x2_send, x2_recv = take(4)
-    z_send, z_recv, g_send, g_recv = take(4)
+    out_sem, x1_recv, x2_recv, z_recv, g_recv = take(5)
 
     rate = n ** (-0.5)
     b = lax.axis_index("batch")
@@ -501,16 +515,9 @@
     def unpack(c, code, terms):
         return code if c == tiny else decode(code, terms * limit)
 
-    def x1_copy(c):
-        return remote(x1_out[c], x1_in[c], x1_send.at[c], x1_recv.at[c], partner)
-
-    def x2_copy(c):
-        return remote(x2_out[c], x2_in[c], x2_send.at[c], x2_recv.at[c], partner)
-
     def program(end, order):
         waited = set()
         sent = []
-        met = []
         out_to = b + 2 * way
         near_to = b - 2 * way
         lines = ("out",) if end else ("near", "out")
@@ -520,12 +527,20 @@
                 waited.add(key)
                 wait()
 
+        def slot():
+            return out_sem.at[len(sent)]
+
         def send(copy):
-            if not met:
-                met.append(True)
+            if not sent:
                 pl.semaphore_wait(barrier, 2 if end else 3)
             copy.start()
             sent.append(copy)
+
+        def x1_copy(c):
+            return remote(x1_out[c], x1_in[c], slot(), x1_recv.at[c], partner)
+
+        def x2_copy(c):
+            return remote(x2_out[c], x2_in[c], slot(), x2_recv.at[c], partner)
 
         def need(c):
             if c < tiny:
@@ -544,17 +559,17 @@
         def z_copy(c, kind):
             m = 2 if plan[c][3] == "Z" else 1
             if kind == "end":
-                lo, size, slot, dst, to = 0, 3 * m, 0, far_in[c], out_to
+                lo, size, dst, to = 0, 3 * m, far_in[c], out_to
             elif kind == "mid":
                 dst = near_in[c].at[pl.ds(0, 2 * m)]
-                lo, size, slot, to = 0, 2 * m, 0, out_to
+                lo, size, to = 0, 2 * m, out_to
             else:
                 dst = near_in[c].at[pl.ds(0, m)]
-                lo, size, slot, to = 2 * m, m, 1, near_to
+                lo, size, to = 2 * m, m, near_to
             return remote(
                 z_out[c].at[pl.ds(lo, size)],
                 dst,
-                z_send.at[slot, c],
+                slot(),
                 z_recv.at[0 if kind == "end" else 1, c],
                 to,
             )
@@ -661,10 +676,15 @@
             own[c][...] = line_sum(c, side)
 
         def block_copy(c, d, lane):
-            to = {"x": partner, "out": out_to, "near": near_to}[lane]
-            slot = {"x": 0, "out": 1, "near": 2}[lane]
+            to = {
+                "x": partner,
+                "out": out_to,
+                "near": near_to,
+                "two": b + 4 * way,
+                "three": b + 6 * way,
+            }[lane]
             ref = block(c, d)
-            return remote(ref, ref, g_send.at[slot, c, d], g_recv.at[c, d], to)
+            return remote(ref, ref, slot(), g_recv.at[c, d], to)
 
         def got(c, step, s):
             d = 2 * (g + way * step) + (1 - side if s else side)
@@ -688,9 +708,10 @@
                     total = total + unpack(c, near_in[c][0], 4)
             if c == tiny:
                 mean = total * rate
-                vec_mine[0:1, :] = norm_master[...] - learn_rate * mean[0:1]
-                vec_mine[1:2, :] = bias_master[...] - learn_rate * mean[1:2]
-                vec_all[b] = vec_mine[...]
+                norm_step[...] = norm_master[...] - learn_rate * mean[0:1]
+                bias_step[...] = bias_master[...] - learn_rate * mean[1:2]
+                vec_all[b, 0:1, :] = norm_step[...]
+                vec_all[b, 1:2, :] = bias_step[...]
             else:
                 k, start, size = plan[c][:3]
                 first(("master", k), masters[k].wait)
@@ -699,13 +720,16 @@
                 stepped[k][rows, :] = new
                 at_rows, at_cols = place(c, b)
                 gathered[k][at_rows, at_cols] = new.astype(jnp.bfloat16)
-            for lane in lines + ("x",):
+            direct = ("three", "two") if end else ("two",)
+            for lane in (direct if plan[c][4] == "D" else ()) + lines + ("x",):
                 send(block_copy(c, b, lane))
 
         def relay(step, s, lanes):
             def go(c):
                 d = got(c, step, s)
-                for lane in lanes if plan[c][4] == "Z" else lanes + ("x",):
+                kind = plan[c][4]
+                lanes_now = (() if kind == "D" else lanes) + (() if kind == "Z" else ("x",))
+                for lane in lanes_now:
                     send(block_copy(c, d, lane))
 
             return go
@@ -731,13 +755,27 @@
             copy.start()
         for c, move in order:
             moves[move](c)
-        for c in range(chunks):
-            for step in (0, 1, 2, 3) if end else (-1, 0, 1, 2):
-                for s in range(2):
-                    if step or s:
-                        got(c, step, s)
+        steps = (0, 1, 2, 3) if end else (-1, 0, 1, 2)
+        left = [(c, k, s) for c in range(chunks) for k in steps for s in (0, 1) if k or s]
+        left.sort(key=lambda x: (x[0] != tiny, when(end, *x)))
+        for c, step, s in left:
+            if c == tiny:
+                got(c, step, s)
+        norm_out[...] = vec_all[:, 0, :].astype(jnp.bfloat16)
+        bias_out[...] = vec_all[:, 1, :].astype(jnp.bfloat16)
         for copy in sent:
             copy.wait_send()
+        for c, step, s in left:
+            got(c, step, s)
+
+    def when(end, c, step, s):
+        own_side = {-1: "rE", 0: "f", 1: "r1" if end else "rM", 2: "r2" if end else "rF", 3: "r3"}
+        if plan[c][4] != "Z" and s:
+            moves, name = orders[0 if end else 1], own_side[step]
+        else:
+            names = {1: ("f", "b0"), 2: ("rM", "sM"), 3: ("rF", "sF")}
+            moves, name = orders[1], names.get(step, ("f", "f"))[s]
+        return moves.index((c, name)) / len(moves) if (c, name) in moves else 0
 
     barrier = pltpu.get_barrier_semaphore()
 
@@ -768,6 +806,23 @@
         copy.wait()
 
 
+def deliver(count, *refs):
+    sources, targets, sem = refs[:count], refs[count:-1], refs[-1]
+    copies = []
+    for i in range(count):
+        rows = sources[i].shape[0]
+        pieces = PIECES if rows >= 128 else 1
+        for k in range(pieces):
+            at = pl.ds(k * (rows // pieces), rows // pieces)
+            copies.append(
+                pltpu.make_async_copy(sources[i].at[at], targets[i].at[at], sem.at[i, k])
+            )
+    for copy in copies:
+        copy.start()
+    for copy in copies:
+        copy.wait()
+
+
 def exchange_ladder(partials, masters, vectors, limit, kinds):
     n = lax.axis_size("batch")
     groups = n // 2
@@ -794,21 +849,23 @@
     chunks = len(plan)
     out_shape = [pltpu.VMEM(p.shape[1:], jnp.bfloat16) for p in partials]
     out_shape += [pltpu.VMEM(m.shape, jnp.float32) for m in masters]
-    out_shape += [pltpu.VMEM((n, 2, w), jnp.float32), pltpu.VMEM((2, w), jnp.float32)]
+    out_shape += [pltpu.VMEM((n, w), jnp.bfloat16)] * 2
+    out_shape += [pltpu.VMEM((1, w), jnp.float32)] * 2
     scratch = buffers(lambda p: (groups if p[3] == "X" else 1,)) * 2
     scratch += line(3) * 2 + line(2)
     scratch += buffers(lambda p: ()) * 2
     scratch += [pltpu.VMEM(s, jnp.float32) for s in shapes]
     scratch += [pltpu.VMEM(p.shape[1:], jnp.float32) for p in partials]
     scratch += [pltpu.VMEM(m.shape, jnp.float32) for m in masters]
-    scratch += [pltpu.VMEM((n, 2, w), jnp.float32)]
+    scratch += [pltpu.VMEM((n, 2, w), jnp.float32)] * 2
     scratch += [pltpu.VMEM((n, 1, w), jnp.float32)] * 2
     scratch += [pltpu.VMEM((1, w), jnp.float32)] * 2
     scratch += [dma((len(partials),))] * 2 + [dma((4,))]
-    scratch += [dma((chunks,))] * 4 + [dma((2, chunks))] * 2
-    scratch += [dma((3, chunks, n)), dma((chunks, n))]
+    sends = sum(3 + {"X": 9, "Z": 11, "D": 7}[p[4]] for p in plan)
+    scratch += [dma((sends,)), dma((chunks,)), dma((chunks,))]
+    scratch += [dma((2, chunks)), dma((chunks, n))]
     args = (*partials, *masters, *vectors)
-    return pl.pallas_call(
+    outs = pl.pallas_call(
         functools.partial(ladder, n, kinds, limit, plan, orders),
         out_shape=out_shape,
         in_specs=[pl.BlockSpec(memory_space=pltpu.HBM)] * len(args),
@@ -818,6 +875,14 @@
             collective_id=0, has_side_effects=True, vmem_limit_bytes=40 << 20
         ),
     )(*(pltpu.with_memory_space_constraint(x, pltpu.HBM) for x in args))
+    return pl.pallas_call(
+        functools.partial(deliver, len(outs)),
+        out_shape=[jax.ShapeDtypeStruct(x.shape, x.dtype) for x in outs],
+        in_specs=[pl.BlockSpec(memory_space=pltpu.VMEM)] * len(outs),
+        out_specs=[pl.BlockSpec(memory_space=pltpu.HBM)] * len(outs),
+        scratch_shapes=[dma((len(outs), PIECES))],
+        compiler_params=pltpu.CompilerParams(vmem_limit_bytes=8 << 20),
+    )(*(pltpu.with_memory_space_constraint(x, pltpu.VMEM) for x in outs))
 
 
 def per_device(
@@ -892,18 +957,18 @@
         outs = exchange_ladder(partials, masters, vectors, limit, kinds)
     else:
         outs = exchange(*(pin(x) for x in (*partials, *masters, *vectors)))
-    large, (vec_all, vec_mine) = outs[:8], outs[8:]
-    tail_shape = [jax.ShapeDtypeStruct(x.shape, x.dtype) for x in large]
-    tail_shape += [jax.ShapeDtypeStruct((n, w), jnp.bfloat16)] * 2
-    tail_shape += [jax.ShapeDtypeStruct((1, w), jnp.float32)] * 2
-    outs = pl.pallas_call(
-        functools.partial(hand_over, len(large)),
-        out_shape=tail_shape,
-        in_specs=[vmem] * (len(large) + 2),
-        out_specs=[hbm] * len(large) + [vmem] * 4,
-        scratch_shapes=[dma((len(large),))],
-        compiler_params=pltpu.CompilerParams(vmem_limit_bytes=8 << 20),
-    )(*(pltpu.with_memory_space_constraint(x, pltpu.VMEM) for x in (*large, vec_all, vec_mine)))
+        large, (vec_all, vec_mine) = outs[:8], outs[8:]
+        tail_shape = [jax.ShapeDtypeStruct(x.shape, x.dtype) for x in large]
+        tail_shape += [jax.ShapeDtypeStruct((n, w), jnp.bfloat16)] * 2
+        tail_shape += [jax.ShapeDtypeStruct((1, w), jnp.float32)] * 2
+        outs = pl.pallas_call(
+            functools.partial(hand_over, len(large)),
+            out_shape=tail_shape,
+            in_specs=[vmem] * (len(large) + 2),
+            out_specs=[hbm] * len(large) + [vmem] * 4,
+            scratch_shapes=[dma((len(large),))],
+            compiler_params=pltpu.CompilerParams(vmem_limit_bytes=8 << 20),
+        )(*(pltpu.with_memory_space_constraint(x, pltpu.VMEM) for x in (*large, vec_all, vec_mine)))
     computes, steppeds, vectors = outs[:4], outs[4:8], outs[8:]
     if not wide:
         computes = (*computes[:3], computes[3].T)

time: 56.8 us -> 53 us (0.933)
  Pallas kernels: 55.9 us -> 52.2 us
    pallas_call x1, Pallas kernels: 53.8 us -> 50.5 us  [exchange_ladder(): pl.pallas_call(functools.partial(ladder, n, kinds, limit, plan, orders),...]
where the time goes in v3:
time: 53 us; the launch traced here: 52.8 us
  Pallas kernels  52.2 us (98%)
  between operations  0.66 us (1%)
    pallas_call x1, Pallas kernels, exchange_ladder(): pl.pallas_call(functools.partial(ladder, n, kinds, limit, plan, orders),...  50.5 us
    pallas_call x1, Pallas kernels, exchange_ladder(): pl.pallas_call(functools.partial(deliver, len(outs)), out_shape=[jax.Shap...  1.7 us

profile of v3, /device:TPU:0, one launch (start us, length us, event | category | flops | bytes accessed | tf_op | source)
XLA Modules:
  0.0 52.8 jit_solution(8987139371110483472)
XLA Ops:
  0.6 50.5 %shard_map.211 = (bf16[1024,256]{1,0:T(8,128)(2,1)S(1)}, bf16[1024,256]{1,0:T(8,128)(2,1)S(1)}, bf16[1024,256]{1,0:T(8,128)(2,1)S(1)}, bf16[256,1024]{1,0:T(8,12...) custom-call(f32[1,1024,256]{2,1,0:T(8,128)} %refs_0_.1, ...), custom_call_target="tpu_custom_call" | custom-call | tf_op jit(solution)/shard_map/pallas_call | solution.py:868
  51.1 1.7 %shard_map.212 = (bf16[1024,256]{1,0:T(8,128)(2,1)}, bf16[1024,256]{1,0:T(8,128)(2,1)}, bf16[1024,256]{1,0:T(8,128)(2,1)}, bf16[256,1024]{1,0:T(8,128)(2,1)}, f3...) custom-call(bf16[1024,256]{1,0:T(8,128)(2,1)S(1)} %get-tuple-element, ...), custom_call_target="tpu_custom_call" | custom-call | tf_op jit(solution)/shard_map/pallas_call | solution.py:878

commit v4 on v3

--- a/solution.py
+++ b/solution.py
@@ -1,4 +1,5 @@
 import functools
+import math
 
 import jax
 import jax.numpy as jnp
@@ -450,7 +451,9 @@
     partial, master = take(count), take(count)
     vec_all, vec_part, norm_part, bias_part, norm_master, bias_master = take(6)
     in_sem, master_sem, small_sem = take(3)
-    out_sem, x1_recv, x2_recv, z_recv, g_recv = take(5)
+    (tally,) = take(1)
+    all_send, leaf_recv, tiny_send, tiny_recv = take(4)
+    x1_recv, x2_recv, z_recv, relay_recv = take(4)
 
     rate = n ** (-0.5)
     b = lax.axis_index("batch")
@@ -465,7 +468,7 @@
         for a in range(count)
     ]
     masters = [
-        pltpu.make_async_copy(master_in[a], master[a], master_sem.at[a])
+        pltpu.make_async_copy(master_in[a], master[a], master_sem.at[0])
         for a in range(count)
     ]
     smalls = [
@@ -517,7 +520,7 @@
 
     def program(end, order):
         waited = set()
-        sent = []
+        sent, tiny_sent = [], []
         out_to = b + 2 * way
         near_to = b - 2 * way
         lines = ("out",) if end else ("near", "out")
@@ -527,20 +530,24 @@
                 waited.add(key)
                 wait()
 
-        def slot():
-            return out_sem.at[len(sent)]
-
-        def send(copy):
-            if not sent:
+        def slot(c):
+            return tiny_send.at[len(tiny_sent)] if c == tiny else all_send.at[0]
+
+        def send(c, copy):
+            if not sent and not tiny_sent:
                 pl.semaphore_wait(barrier, 2 if end else 3)
             copy.start()
-            sent.append(copy)
+            (tiny_sent if c == tiny else sent).append(copy)
+
+        def settle(rows):
+            ref = tally.at[pl.ds(0, rows)]
+            return remote(ref, ref, all_send.at[0], leaf_recv.at[0], partner)
 
         def x1_copy(c):
-            return remote(x1_out[c], x1_in[c], slot(), x1_recv.at[c], partner)
+            return remote(x1_out[c], x1_in[c], slot(c), x1_recv.at[c], partner)
 
         def x2_copy(c):
-            return remote(x2_out[c], x2_in[c], slot(), x2_recv.at[c], partner)
+            return remote(x2_out[c], x2_in[c], slot(c), x2_recv.at[c], partner)
 
         def need(c):
             if c < tiny:
@@ -569,7 +576,7 @@
             return remote(
                 z_out[c].at[pl.ds(lo, size)],
                 dst,
-                slot(),
+                slot(c),
                 z_recv.at[0 if kind == "end" else 1, c],
                 to,
             )
@@ -600,7 +607,7 @@
                 x1_out[c][z] = pack(c, load(c, 2 * z + 1 - side), 1)
 
             each(0, groups, put)
-            send(x1_copy(c))
+            send(c, x1_copy(c))
 
         def z0(c):
             need(c)
@@ -618,7 +625,7 @@
                     z_out[c][j] = pack(c, pair(c, g + way * (j + 1)), 2)
 
                 each(0, 3, put)
-            send(z_copy(c, "end"))
+            send(c, z_copy(c, "end"))
 
         def a(c):
             need(c)
@@ -640,7 +647,7 @@
                     z_out[c][j] = pack(c, total, 4)
 
                 each(0, 2, put)
-            send(z_copy(c, "mid"))
+            send(c, z_copy(c, "mid"))
 
         def back(c):
             need(c)
@@ -658,7 +665,7 @@
                 got_near(c)
                 total = pair(c, z) + unpack(c, near_in[c][1], 4)
                 z_out[c][2] = pack(c, total, 6)
-            send(z_copy(c, "back"))
+            send(c, z_copy(c, "back"))
 
         def line_sum(c, s):
             total = load(c, 2 * g + s)
@@ -672,10 +679,22 @@
             if not end:
                 got_far(c)
             x2_out[c][...] = pack(c, line_sum(c, 1 - side), 4)
-            send(x2_copy(c))
+            send(c, x2_copy(c))
             own[c][...] = line_sum(c, side)
 
-        def block_copy(c, d, lane):
+        def arrival(c, here, step, s):
+            if c == tiny:
+                return tiny_recv.at[2 * (g + way * step) + (1 - side if s else side)]
+            kind = plan[c][4]
+            if (kind == "Z" and here) if step or not s else kind != "Z":
+                return leaf_recv.at[0]
+            if kind != "Z" and s:
+                return leaf_recv.at[0]
+            base = sum(7 if p[4] == "Z" else 3 for p in plan[:c])
+            at = {-1: 0, 1: 1, 2: 2} if not here else {1: 0, 2: 1, 3: 2}
+            return relay_recv.at[base + (6 if s and not step else at[step] + 3 * s)]
+
+        def block_copy(c, d, lane, step, s):
             to = {
                 "x": partner,
                 "out": out_to,
@@ -683,13 +702,34 @@
                 "two": b + 4 * way,
                 "three": b + 6 * way,
             }[lane]
+            if lane == "x":
+                there, step_there, s_there = end, step, 1 - s
+            elif end:
+                there = lane == "three"
+                step_there, s_there = {"out": -1, "two": 2, "three": 3}[lane], s
+            elif lane == "near":
+                there, step_there, s_there = True, step + 1, s
+            else:
+                there = lane == "two"
+                step_there, s_there = {"out": 1 - step, "two": 2}[lane], s
             ref = block(c, d)
-            return remote(ref, ref, slot(), g_recv.at[c, d], to)
+            if c == tiny:
+                recv = tiny_recv.at[d]
+            else:
+                recv = arrival(c, there, step_there, s_there)
+            return remote(ref, ref, slot(c), recv, to)
 
         def got(c, step, s):
             d = 2 * (g + way * step) + (1 - side if s else side)
-            first(("block", c, step, s), block_copy(c, d, "x").wait_recv)
+            ref = block(c, d)
+            copy = remote(ref, ref, slot(c), arrival(c, end, step, s), partner)
+            first(("block", c, step, s), copy.wait_recv)
             return d
+
+        def leaf(c, step, s):
+            if plan[c][4] == "Z":
+                return end and step != 0
+            return s == 1
 
         def f(c):
             need(c)
@@ -714,7 +754,12 @@
                 vec_all[b, 1:2, :] = bias_step[...]
             else:
                 k, start, size = plan[c][:3]
-                first(("master", k), masters[k].wait)
+                half = partial[0].shape[0] // 2
+                first("master", lambda: pltpu.make_async_copy(
+                    partial[0].at[pl.ds(0, half)],
+                    partial[1].at[pl.ds(0, half)],
+                    master_sem.at[0],
+                ).wait())
                 rows = pl.ds(start, size)
                 new = master[k][rows, :] - learn_rate * (total * rate)
                 stepped[k][rows, :] = new
@@ -722,7 +767,7 @@
                 gathered[k][at_rows, at_cols] = new.astype(jnp.bfloat16)
             direct = ("three", "two") if end else ("two",)
             for lane in (direct if plan[c][4] == "D" else ()) + lines + ("x",):
-                send(block_copy(c, b, lane))
+                send(c, block_copy(c, b, lane, 0, 0))
 
         def relay(step, s, lanes):
             def go(c):
@@ -730,7 +775,7 @@
                 kind = plan[c][4]
                 lanes_now = (() if kind == "D" else lanes) + (() if kind == "Z" else ("x",))
                 for lane in lanes_now:
-                    send(block_copy(c, d, lane))
+                    send(c, block_copy(c, d, lane, step, s))
 
             return go
 
@@ -757,25 +802,21 @@
             moves[move](c)
         steps = (0, 1, 2, 3) if end else (-1, 0, 1, 2)
         left = [(c, k, s) for c in range(chunks) for k in steps for s in (0, 1) if k or s]
-        left.sort(key=lambda x: (x[0] != tiny, when(end, *x)))
         for c, step, s in left:
-            if c == tiny:
+            if c == tiny or not leaf(c, step, s):
                 got(c, step, s)
         norm_out[...] = vec_all[:, 0, :].astype(jnp.bfloat16)
         bias_out[...] = vec_all[:, 1, :].astype(jnp.bfloat16)
-        for copy in sent:
+        for copy in tiny_sent:
             copy.wait_send()
-        for c, step, s in left:
-            got(c, step, s)
-
-    def when(end, c, step, s):
-        own_side = {-1: "rE", 0: "f", 1: "r1" if end else "rM", 2: "r2" if end else "rF", 3: "r3"}
-        if plan[c][4] != "Z" and s:
-            moves, name = orders[0 if end else 1], own_side[step]
-        else:
-            names = {1: ("f", "b0"), 2: ("rM", "sM"), 3: ("rF", "sF")}
-            moves, name = orders[1], names.get(step, ("f", "f"))[s]
-        return moves.index((c, name)) / len(moves) if (c, name) in moves else 0
+        row = tally.shape[1] * 4
+
+        def nbytes(ref):
+            return math.prod(ref.shape) * 2
+
+        settle(sum(nbytes(copy.src_ref) for copy in sent) // row).wait_send()
+        last = [nbytes(block(c, 0)) for c, step, s in left if c != tiny and leaf(c, step, s)]
+        settle(sum(last) // row).wait_recv()
 
     barrier = pltpu.get_barrier_semaphore()
 
@@ -860,10 +901,12 @@
     scratch += [pltpu.VMEM((n, 2, w), jnp.float32)] * 2
     scratch += [pltpu.VMEM((n, 1, w), jnp.float32)] * 2
     scratch += [pltpu.VMEM((1, w), jnp.float32)] * 2
-    scratch += [dma((len(partials),))] * 2 + [dma((4,))]
-    sends = sum(3 + {"X": 9, "Z": 11, "D": 7}[p[4]] for p in plan)
-    scratch += [dma((sends,)), dma((chunks,)), dma((chunks,))]
-    scratch += [dma((2, chunks)), dma((chunks, n))]
+    rows = 18 * sum(m.size for m in masters) // 512
+    scratch += [dma((len(partials),)), dma((1,)), dma((4,))]
+    scratch += [pltpu.VMEM((rows, 256), jnp.float32)]
+    scratch += [dma((1,)), dma((1,)), dma((12,)), dma((n,))]
+    relays = sum(7 if p[4] == "Z" else 3 for p in plan)
+    scratch += [dma((chunks,)), dma((chunks,)), dma((2, chunks)), dma((relays,))]
     args = (*partials, *masters, *vectors)
     outs = pl.pallas_call(
         functools.partial(ladder, n, kinds, limit, plan, orders),

time: 53 us -> 51.7 us (0.975)
  Pallas kernels: 52.2 us -> 50.8 us
    pallas_call x1, Pallas kernels: 50.5 us -> 49.1 us  [exchange_ladder(): pl.pallas_call(functools.partial(ladder, n, kinds, limit, plan, orders),...]
where the time goes in v4:
time: 51.7 us; the launch traced here: 51.5 us
  Pallas kernels  50.8 us (98%)
  between operations  0.66 us (1%)
    pallas_call x1, Pallas kernels, exchange_ladder(): pl.pallas_call(functools.partial(ladder, n, kinds, limit, plan, orders),...  49.1 us
    pallas_call x1, Pallas kernels, exchange_ladder(): pl.pallas_call(functools.partial(deliver, len(outs)), out_shape=[jax.Shap...  1.7 us

profile of v4, /device:TPU:0, one launch (start us, length us, event | category | flops | bytes accessed | tf_op | source)
XLA Modules:
  0.0 51.5 jit_solution(16298092857907620561)
XLA Ops:
  0.6 49.1 %shard_map.211 = (bf16[1024,256]{1,0:T(8,128)(2,1)S(1)}, bf16[1024,256]{1,0:T(8,128)(2,1)S(1)}, bf16[1024,256]{1,0:T(8,128)(2,1)S(1)}, bf16[256,1024]{1,0:T(8,12...) custom-call(f32[1,1024,256]{2,1,0:T(8,128)} %refs_0_.1, ...), custom_call_target="tpu_custom_call" | custom-call | tf_op jit(solution)/shard_map/pallas_call | solution.py:911
  49.8 1.7 %shard_map.212 = (bf16[1024,256]{1,0:T(8,128)(2,1)}, bf16[1024,256]{1,0:T(8,128)(2,1)}, bf16[1024,256]{1,0:T(8,128)(2,1)}, bf16[256,1024]{1,0:T(8,128)(2,1)}, f3...) custom-call(bf16[1024,256]{1,0:T(8,128)(2,1)S(1)} %get-tuple-element, ...), custom_call_target="tpu_custom_call" | custom-call | tf_op jit(solution)/shard_map/pallas_call | solution.py:921

commit v5 on v4

--- a/solution.py
+++ b/solution.py
@@ -547,7 +547,8 @@
             return remote(x1_out[c], x1_in[c], slot(c), x1_recv.at[c], partner)
 
         def x2_copy(c):
-            return remote(x2_out[c], x2_in[c], slot(c), x2_recv.at[c], partner)
+            at = sum(p[3] == "Z" for p in plan[:c])
+            return remote(x2_out[c], x2_in[c], slot(c), x2_recv.at[at], partner)
 
         def need(c):
             if c < tiny:
@@ -847,21 +848,24 @@
         copy.wait()
 
 
-def deliver(count, *refs):
-    sources, targets, sem = refs[:count], refs[count:-1], refs[-1]
+def deliver(large, count, *refs):
+    sources, targets = refs[:count], refs[count : 2 * count]
+    tally, sem = refs[2 * count :]
     copies = []
     for i in range(count):
         rows = sources[i].shape[0]
-        pieces = PIECES if rows >= 128 else 1
+        pieces = PIECES if i < large else 1
         for k in range(pieces):
             at = pl.ds(k * (rows // pieces), rows // pieces)
+            which = 0 if i < large else 1 + i - large
             copies.append(
-                pltpu.make_async_copy(sources[i].at[at], targets[i].at[at], sem.at[i, k])
+                pltpu.make_async_copy(sources[i].at[at], targets[i].at[at], sem.at[which])
             )
     for copy in copies:
         copy.start()
-    for copy in copies:
+    for copy in copies[large * PIECES :]:
         copy.wait()
+    pltpu.make_async_copy(tally, tally, sem.at[0]).wait()
 
 
 def exchange_ladder(partials, masters, vectors, limit, kinds):
@@ -906,7 +910,8 @@
     scratch += [pltpu.VMEM((rows, 256), jnp.float32)]
     scratch += [dma((1,)), dma((1,)), dma((12,)), dma((n,))]
     relays = sum(7 if p[4] == "Z" else 3 for p in plan)
-    scratch += [dma((chunks,)), dma((chunks,)), dma((2, chunks)), dma((relays,))]
+    crossed = max(1, sum(p[3] == "Z" for p in plan))
+    scratch += [dma((chunks,)), dma((crossed,)), dma((2, chunks)), dma((relays,))]
     args = (*partials, *masters, *vectors)
     outs = pl.pallas_call(
         functools.partial(ladder, n, kinds, limit, plan, orders),
@@ -918,12 +923,14 @@
             collective_id=0, has_side_effects=True, vmem_limit_bytes=40 << 20
         ),
     )(*(pltpu.with_memory_space_constraint(x, pltpu.HBM) for x in args))
+    large = 2 * len(partials)
+    rows = sum(math.prod(x.shape) * x.dtype.itemsize for x in outs[:large]) // 1024
     return pl.pallas_call(
-        functools.partial(deliver, len(outs)),
+        functools.partial(deliver, large, len(outs)),
         out_shape=[jax.ShapeDtypeStruct(x.shape, x.dtype) for x in outs],
         in_specs=[pl.BlockSpec(memory_space=pltpu.VMEM)] * len(outs),
         out_specs=[pl.BlockSpec(memory_space=pltpu.HBM)] * len(outs),
-        scratch_shapes=[dma((len(outs), PIECES))],
+        scratch_shapes=[pltpu.VMEM((rows, 256), jnp.float32), dma((5,))],
         compiler_params=pltpu.CompilerParams(vmem_limit_bytes=8 << 20),
     )(*(pltpu.with_memory_space_constraint(x, pltpu.VMEM) for x in outs))
 

time: 51.7 us -> 51.4 us (level)
  no operation moved by 1% of the time
where the time goes in v5:
time: 51.4 us; the launch traced here: 51.2 us
  Pallas kernels  50.6 us (98%)
  between operations  0.66 us (1%)
    pallas_call x1, Pallas kernels, exchange_ladder(): pl.pallas_call(functools.partial(ladder, n, kinds, limit, plan, orders),...  49.1 us
    pallas_call x1, Pallas kernels, exchange_ladder(): pl.pallas_call(functools.partial(deliver, large, len(outs)), out_shape=[j...  1.52 us

profile of v5, /device:TPU:0, one launch (start us, length us, event | category | flops | bytes accessed | tf_op | source)
XLA Modules:
  0.0 51.2 jit_solution(10727721876347869923)
XLA Ops:
  0.6 49.1 %shard_map.211 = (bf16[1024,256]{1,0:T(8,128)(2,1)S(1)}, bf16[1024,256]{1,0:T(8,128)(2,1)S(1)}, bf16[1024,256]{1,0:T(8,128)(2,1)S(1)}, bf16[256,1024]{1,0:T(8,12...) custom-call(f32[1,1024,256]{2,1,0:T(8,128)} %refs_0_.1, ...), custom_call_target="tpu_custom_call" | custom-call | tf_op jit(solution)/shard_map/pallas_call | solution.py:916
  49.7 1.5 %shard_map.212 = (bf16[1024,256]{1,0:T(8,128)(2,1)}, bf16[1024,256]{1,0:T(8,128)(2,1)}, bf16[1024,256]{1,0:T(8,128)(2,1)}, bf16[256,1024]{1,0:T(8,128)(2,1)}, f3...) custom-call(bf16[1024,256]{1,0:T(8,128)(2,1)S(1)} %get-tuple-element, ...), custom_call_target="tpu_custom_call" | custom-call | tf_op jit(solution)/shard_map/pallas_call | solution.py:928
